TPU v7x, 32 devices: a whole 2x2x4 slice. The times are simulated.
32 devices in a mesh: expert: 8 (over z, core), latent: 2 (over y), row: 2 (over x).
Axes of the slice: x: 2, y: 2, z: 4, core: 2. Of those that a mesh axis runs over, the one named last changes fastest.
Arguments:
- model_acts: bfloat16 [512, 8192], P('row', 'expert'), may hold values from -6 to 6
- enc_weight: bfloat16 [8192, 12288], P('expert', ('latent', 'row')), may hold values from -0.0625 to 0.0625
- dec_weight: bfloat16 [12288, 8192], P(('latent', 'row'), 'expert'), may hold values from -0.0546875 to 0.0546875
- enc_bias: float32 [12288], P('latent'), may hold values from -3 to 3
- dec_bias: float32 [8192], P('expert'), may hold values from -3 to 3
- enc_first: bfloat16 [8192, 12288], P('expert', ('latent', 'row')), may hold values from -0.119628906 to 0.119628906
- enc_second: bfloat16 [8192, 12288], P('expert', ('latent', 'row')), may hold values from 9.9658966e-05 to 0.0099487305
- dec_first: bfloat16 [12288, 8192], P(('latent', 'row'), 'expert'), may hold values from -0.119628906 to 0.119628906
- dec_second: bfloat16 [12288, 8192], P(('latent', 'row'), 'expert'), may hold values from 9.9658966e-05 to 0.0099487305
Outputs:
- encoder_next: bfloat16 [8192, 12288], P('expert', ('latent', 'row'))
- decoder_next: bfloat16 [12288, 8192], P(('latent', 'row'), 'expert')
- enc_first_next: bfloat16 [8192, 12288], P('expert', ('latent', 'row'))
- enc_second_next: bfloat16 [8192, 12288], P('expert', ('latent', 'row'))
- dec_first_next: bfloat16 [12288, 8192], P(('latent', 'row'), 'expert')
- dec_second_next: bfloat16 [12288, 8192], P(('latent', 'row'), 'expert')
- enc_bias_grad: float32 [12288], P(('latent', 'row'))
- dec_bias_grad: float32 [8192], P('expert')
All inputs are finite; a program needn't handle non-finite values.
Results may differ from a plain program's by a relative error of at most 0.005.
Values may be sent and summed in bfloat16 or wider, within the bound.
No kernel may reach another device: no remote copies, remote signals or barrier semaphores. Data moves between devices by JAX's collectives and lax.ppermute only.
A program may use at most 128 MiB of HBM per device.

v0:
```python
import jax
import jax.numpy as jnp
from jax import lax
from jax.sharding import PartitionSpec as P

EXPERTS = 8
D = 1024
beta_one = 0.9
beta_two = 0.999
learn_rate = 0.001
adam_eps = 1e-08
bias_one = 0.9999734386011124
bias_two = 0.09520785288629115
norm_eps = 1e-06
sparsity = 1.0


def adam_step(weight, moment_one, moment_two, gradient):
    first_next = beta_one * moment_one.astype(jnp.float32) + (1.0 - beta_one) * gradient
    second_next = beta_two * moment_two.astype(jnp.float32) + (1.0 - beta_two) * gradient * gradient
    stepped = weight.astype(jnp.float32) - learn_rate * (first_next / bias_one) / (
        jnp.sqrt(second_next / bias_two) + adam_eps
    )
    return (
        stepped.astype(jnp.bfloat16),
        first_next.astype(jnp.bfloat16),
        second_next.astype(jnp.bfloat16),
    )


def contract_rows(left, right):
    return lax.dot_general(
        left, right, (((0,), (0,)), ((), ())), preferred_element_type=jnp.float32
    )


def local(
    model_acts,
    enc_weight,
    dec_weight,
    enc_bias,
    dec_bias,
    enc_first,
    enc_second,
    dec_first,
    dec_second,
):
    shard_width = model_acts.shape[1]
    local_latents = enc_weight.shape[1]
    total_rows = model_acts.shape[0] * lax.axis_size("row")
    row_index = lax.axis_index("row")
    token_rows = lax.all_gather(model_acts, "row", axis=0, tiled=True)
    bias_here = lax.dynamic_slice_in_dim(enc_bias, row_index * local_latents, local_latents)
    column_pick = (jnp.arange(EXPERTS) == lax.axis_index("expert") * shard_width // D).astype(
        jnp.float32
    )
    decoder_wide = dec_weight.astype(jnp.float32)
    partial_sq = jnp.sum(decoder_wide * decoder_wide, axis=1)
    norm_sq = lax.psum(partial_sq[:, None] * column_pick[None, :], "expert")
    decoder_norms = jnp.sqrt(norm_sq + norm_eps)
    strength = jnp.sum(decoder_norms, axis=1)
    own_norm = jnp.sum(decoder_norms * column_pick[None, :], axis=1)
    preact_part = jnp.dot(token_rows, enc_weight, preferred_element_type=jnp.float32)
    preact = lax.psum_scatter(preact_part, "expert", scatter_dimension=0, tiled=True) + bias_here
    active = preact > 0
    latent_low = lax.all_gather(
        jnp.maximum(preact, 0.0).astype(jnp.bfloat16), "expert", axis=0, tiled=True
    )
    rebuilt_part = jnp.dot(latent_low, dec_weight, preferred_element_type=jnp.float32)
    rebuilt = lax.psum(rebuilt_part, ("latent", "row"))
    grad_rows = 2.0 * (rebuilt + dec_bias - token_rows.astype(jnp.float32)) / total_rows
    grad_low = grad_rows.astype(jnp.bfloat16)
    dec_main = contract_rows(latent_low, grad_low)
    col_total = jnp.sum(latent_low.astype(jnp.float32), axis=0)
    row_bias = jnp.sum(grad_rows, axis=0)
    back_part = lax.dot_general(
        grad_low, dec_weight, (((1,), (1,)), ((), ())), preferred_element_type=jnp.float32
    )
    penalty = sparsity * strength / total_rows
    back_grad = lax.psum_scatter(back_part, "expert", scatter_dimension=0, tiled=True) + penalty
    grad_pre = lax.all_gather(
        jnp.where(active, back_grad, 0.0).astype(jnp.bfloat16), "expert", axis=0, tiled=True
    )
    enc_main = contract_rows(token_rows, grad_pre)
    bias_sum = jnp.sum(grad_pre.astype(jnp.float32), axis=0)
    dec_grad = dec_main + sparsity * (col_total / total_rows)[:, None] * (
        dec_weight.astype(jnp.float32) / own_norm[:, None]
    )
    encoder_next, enc_first_next, enc_second_next = adam_step(
        enc_weight, enc_first, enc_second, enc_main
    )
    decoder_next, dec_first_next, dec_second_next = adam_step(
        dec_weight, dec_first, dec_second, dec_grad
    )
    return (
        encoder_next,
        decoder_next,
        enc_first_next,
        enc_second_next,
        dec_first_next,
        dec_second_next,
        bias_sum,
        row_bias,
    )


def solution(mesh):
    return jax.shard_map(
        local,
        mesh=mesh,
        in_specs=(
            P("row", "expert"),
            P("expert", ("latent", "row")),
            P(("latent", "row"), "expert"),
            P("latent"),
            P("expert"),
            P("expert", ("latent", "row")),
            P("expert", ("latent", "row")),
            P(("latent", "row"), "expert"),
            P(("latent", "row"), "expert"),
        ),
        out_specs=(
            P("expert", ("latent", "row")),
            P(("latent", "row"), "expert"),
            P("expert", ("latent", "row")),
            P("expert", ("latent", "row")),
            P(("latent", "row"), "expert"),
            P(("latent", "row"), "expert"),
            P(("latent", "row")),
            P("expert"),
        ),
        check_vma=False,
    )
```

profile of v0, /device:TPU:0, one launch (start us, length us, event | category | flops | bytes accessed | tf_op | source)
XLA Modules:
  0.0 464.4 jit_solution(15385568085803733185)
XLA Ops:
  7.9 25.6 %all-gather.4.cloned.1.call-done = bf16[512,1024]{1,0:T(8,128)(2,1)} async-done(((bf16[256,1024]{1,0:T(8,128)(2,1)}), bf16[512,1024]{1,0:T(8,128)(2,1)}) %all-gather.4.cloned.1.call-update) | async-done | bytes 1048592 | tf_op jit(solution)/shard_map/all_gather | solution.py:52
  33.6 9.2 %fusion.14 = f32[512,3072]{1,0:T(8,128)} fusion(bf16[512,1024]{1,0:T(8,128)(2,1)} %all-gather.4.cloned.1.call-done, bf16[1024,3072]{1,0:T(8,128)(2,1)} %param.10), kind=kOutput, calls=%fused_computation.33 | convolution fusion | flops 3221225472 | bytes 13631488 | tf_op jit(solution)/shard_map/dot_general | solution.py:63
  43.5 69.2 %reduce-scatter.3.cloned.1.call-done = f32[64,3072]{1,0:T(8,128)} async-done(((f32[512,3072]{1,0:T(8,128)}), f32[64,3072]{1,0:T(8,128)}) %reduce-scatter.3.cloned.1.call-update) | async-done | bytes 786448 | tf_op jit(solution)/shard_map/reduce_scatter | solution.py:64
  112.7 1.9 maximum_convert_fusion
  114.7 36.9 %all-gather.6.cloned.1.call-done = bf16[512,3072]{1,0:T(8,128)(2,1)} async-done(((bf16[64,3072]{1,0:T(8,128)(2,1)}), bf16[512,3072]{1,0:T(8,128)(2,1)}) %all-gather.6.cloned.1.call-update) | async-done | bytes 3145744 | tf_op jit(solution)/shard_map/all_gather | solution.py:66
  151.7 8.5 %fusion.15 = f32[512,1024]{1,0:T(8,128)} fusion(bf16[512,3072]{1,0:T(8,128)(2,1)} %all-gather.6.cloned.1.call-done, bf16[3072,1024]{1,0:T(8,128)(2,1)} %param.11), kind=kOutput, calls=%fused_computation.34 | convolution fusion | flops 3221225472 | bytes 11534336 | tf_op jit(solution)/shard_map/dot_general | solution.py:69
  160.2 4.2 fusion
  165.2 63.5 %all-reduce.3.cloned.1.call-done = f32[512,1024]{1,0:T(8,128)} async-done(((f32[512,1024]{1,0:T(8,128)}), f32[512,1024]{1,0:T(8,128)}) %all-reduce.3.cloned.1.call-update) | async-done | bytes 2097168 | tf_op jit(solution)/shard_map/psum | solution.py:70
  228.7 2.6 fusion.11
  231.3 1.0 copy-done.4
  232.3 8.2 %fusion.16 = f32[512,3072]{1,0:T(8,128)} fusion(bf16[512,1024]{1,0:T(8,128)(2,1)S(1)} %get-tuple-element.33, bf16[3072,1024]{1,0:T(8,128)(2,1)} %param.11), kind=kOutput, calls=%fused_computation.35 | convolution fusion | flops 3221225472 | bytes 13631488 | tf_op jit(solution)/shard_map/dot_general | solution.py:76
  240.6 43.2 %all-reduce.5.cloned.1.call-done = f32[3072,8]{0,1:T(8,128)} async-done(((f32[3072,8]{0,1:T(8,128)}), f32[3072,8]{0,1:T(8,128)}) %all-reduce.5.cloned.1.call-update) | async-done | bytes 98320 | tf_op jit(solution)/shard_map/psum | solution.py:59
  283.9 1.0 multiply_reduce_fusion
  284.9 73.1 %reduce-scatter.5.cloned.1.call-done = f32[64,3072]{1,0:T(8,128)} async-done(((f32[512,3072]{1,0:T(8,128)}), f32[64,3072]{1,0:T(8,128)}) %reduce-scatter.5.cloned.1.call-update) | async-done | bytes 786448 | tf_op jit(solution)/shard_map/reduce_scatter | solution.py:80
  357.9 2.0 select_convert_fusion
  360.0 8.9 %copy.23 = bf16[1024,3072]{0,1:T(8,128)(2,1)} copy(bf16[1024,3072]{1,0:T(8,128)(2,1)} %param.10) | data formatting | bytes 12582912 | tf_op args[1]
  368.9 8.6 %copy.24 = bf16[1024,3072]{0,1:T(8,128)(2,1)} copy(bf16[1024,3072]{1,0:T(8,128)(2,1)} %param.14) | data formatting | bytes 12582912 | tf_op args[5]
  377.5 8.8 %copy.25 = bf16[1024,3072]{0,1:T(8,128)(2,1)} copy(bf16[1024,3072]{1,0:T(8,128)(2,1)} %param.15) | data formatting | bytes 12582912 | tf_op args[6]
  387.0 21.2 %fusion.9 = (bf16[3072,1024]{1,0:T(8,128)(2,1)}, bf16[3072,1024]{1,0:T(8,128)(2,1)}, bf16[3072,1024]{1,0:T(8,128)(2,1)}) fusion(bf16[3072,1024]{1,0:T(8,128)(2,1)} %param.17, bf16[3072,1024]{1,0:T(8,128)(2,1)} %param.16, bf16[3072,1024]{1,0:T(8,128)(2,1)} %param.11, f32[3072]{0:T(1024)S(1)} %get-tuple-element.24, f32[3072]{0:T(1024)S(1)} %broadcast_multiply_fusion.1, ...), kind=kOutput, calls=%fused_computation.17 | convolution fusion | flops 3287285760 | bytes 41967616 | tf_op jit(solution)/shard_map/dot_general | solution.py:32
  408.2 22.1 %fusion.10 = (bf16[1024,3072]{0,1:T(8,128)(2,1)}, bf16[1024,3072]{0,1:T(8,128)(2,1)}, bf16[1024,3072]{0,1:T(8,128)(2,1)}) fusion(bf16[1024,3072]{0,1:T(8,128)(2,1)} %copy.25, bf16[1024,3072]{0,1:T(8,128)(2,1)} %copy.24, bf16[1024,3072]{0,1:T(8,128)(2,1)} %copy.23, bf16[512,3072]{1,0:T(8,128)(2,1)} %all-gather.8.cloned.1.call-done, ...), kind=kOutput, calls=%fused_computation.18 | convolution fusion | flops 3277848576 | bytes 41943040 | tf_op jit(solution)/shard_map/dot_general | solution.py:32
  430.3 8.6 %copy.28 = bf16[1024,3072]{1,0:T(8,128)(2,1)} copy(bf16[1024,3072]{0,1:T(8,128)(2,1)} %get-tuple-element.29) | data formatting | bytes 12582912
  438.9 8.6 %copy.26 = bf16[1024,3072]{1,0:T(8,128)(2,1)} copy(bf16[1024,3072]{0,1:T(8,128)(2,1)} %get-tuple-element.30) | data formatting | bytes 12582912
  447.6 8.8 %copy.27 = bf16[1024,3072]{1,0:T(8,128)(2,1)} copy(bf16[1024,3072]{0,1:T(8,128)(2,1)} %get-tuple-element.31) | data formatting | bytes 12582912
  456.3 1.2 convert_reduce_fusion
  (34 shorter events, 3.1 us)
Async XLA Ops:
  7.2 26.4 %all-gather.4.cloned.1.call-start = ((), (), s32[]{:S(2)}) async-start(), calls=%async_computation.2 | async-start | bytes 1572864 | tf_op jit(solution)/shard_map/all_gather | solution.py:52
  7.9 104.8 %reduce-scatter.3.cloned.1.call-start = ((), (), s32[]{:S(2)}) async-start(), calls=%async_computation.3 | async-start | bytes 7077888 | tf_op jit(solution)/shard_map/reduce_scatter | solution.py:64
  42.8 0.7 copy-start.5
  42.8 108.8 %all-gather.6.cloned.1.call-start = ((), (), s32[]{:S(2)}) async-start(), calls=%async_computation.4 | async-start | bytes 3538944 | tf_op jit(solution)/shard_map/all_gather | solution.py:66
  114.7 114.0 %all-reduce.3.cloned.1.call-start = ((), (), s32[]{:S(2)}) async-start(), calls=%async_computation.5 | async-start | bytes 4194304 | tf_op jit(solution)/shard_map/psum | solution.py:70
  160.1 68.6 %copy-start.3 = (bf16[512,1024]{1,0:T(8,128)(2,1)S(1)}, bf16[512,1024]{1,0:T(8,128)(2,1)}, u32[]{:S(2)}) copy-start(bf16[512,1024]{1,0:T(8,128)(2,1)} %all-gather.4.cloned.1.call-done) | copy-start | bytes 3145732
  160.1 68.6 %copy-start.6 = (f32[1024]{0:T(1024)S(1)}, f32[1024]{0:T(1024)}, u32[]{:S(2)}) copy-start(f32[1024]{0:T(1024)} %param.13) | copy-start | bytes 12292
  160.2 123.7 %all-reduce.5.cloned.1.call-start = ((), (), s32[]{:S(2)}) async-start(), calls=%async_computation.7 | async-start | bytes 196608 | tf_op jit(solution)/shard_map/psum | solution.py:59
  165.1 192.8 %reduce-scatter.5.cloned.1.call-start = ((), (), s32[]{:S(2)}) async-start(), calls=%async_computation.6 | async-start | bytes 7077888 | tf_op jit(solution)/shard_map/reduce_scatter | solution.py:80
  231.3 1.0 copy-start.4
  240.5 117.4 %copy-start.2 = (f32[64,3072]{1,0:T(8,128)S(1)}, f32[64,3072]{1,0:T(8,128)}, u32[]{:S(2)}) copy-start(f32[64,3072]{1,0:T(8,128)} %reduce-scatter.3.cloned.1.call-done) | copy-start | bytes 2359300
  240.6 167.6 %all-gather.8.cloned.1.call-start = ((), (), s32[]{:S(2)}) async-start(), calls=%async_computation.8 | async-start | bytes 3538944 | tf_op jit(solution)/shard_map/all_gather | solution.py:81
  377.5 8.8 %copy-start = (bf16[512,3072]{1,0:T(8,128)(2,1)S(1)}, bf16[512,3072]{1,0:T(8,128)(2,1)}, u32[]{:S(2)}) copy-start(bf16[512,3072]{1,0:T(8,128)(2,1)} %all-gather.6.cloned.1.call-done) | copy-start | bytes 9437188
  447.6 8.8 %copy-start.1 = (bf16[512,3072]{1,0:T(8,128)(2,1)S(1)}, bf16[512,3072]{1,0:T(8,128)(2,1)}, u32[]{:S(2)}) copy-start(bf16[512,3072]{1,0:T(8,128)(2,1)} %all-gather.8.cloned.1.call-done) | copy-start | bytes 9437188
Sparse Core Ops, SparseCore 0:
  9.5 23.9 all-gather.3
  42.9 69.7 reduce-scatter.2
  114.9 36.6 all-gather.5
  160.3 68.3 all-reduce.2
  231.4 52.3 all-reduce.4
  286.6 71.3 reduce-scatter.4
  360.1 36.6 all-gather.7
where the time goes:
time: 466 us; the launch traced here: 464 us
  waiting for transfers between devices  312 us (67%)
  matrix products  69.3 us (15%)
  local copies, waits for them, and re-layouts  54 us (12%)
  other arithmetic  14.3 us (3%)
  between operations  14.2 us (3%)
    reduce_scatter x1, waiting for transfers between devices, local(): lax.psum_scatter(back_part, 'expert', scatter_dimension=0, tiled=True)  73.1 us
    reduce_scatter x1, waiting for transfers between devices, local(): lax.psum_scatter(preact_part, 'expert', scatter_dimension=0, tiled=True)  69.2 us
    psum x1, waiting for transfers between devices, local(): rebuilt = lax.psum(rebuilt_part, ('latent', 'row'))  63.5 us
    unnamed x20, local copies, waits for them, and re-layouts  54 us
    dot_general x2, matrix products, contract_rows(): lax.dot_general(left, right, (((0,), (0,)), ((), ())), preferred_element_...  43.4 us
    psum x1, waiting for transfers between devices, local(): norm_sq = lax.psum(partial_sq[:, None] * column_pick[None, :], 'expert')  43.2 us
    all_gather x1, waiting for transfers between devices, local(): lax.all_gather(jnp.maximum(preact, 0.0).astype(jnp.bfloat16), 'expert', a...  36.9 us
    all_gather x1, waiting for transfers between devices, local(): token_rows = lax.all_gather(model_acts, 'row', axis=0, tiled=True)  25.6 us
  transfers between devices with their start and end apart: 7, of which 6 were waited for; matrix products, arithmetic and copies ran while one was open for 14% of the time, Pallas kernels for 0%

commit v1 on v0

--- a/solution.py
+++ b/solution.py
@@ -67,7 +67,7 @@
         jnp.maximum(preact, 0.0).astype(jnp.bfloat16), "expert", axis=0, tiled=True
     )
     rebuilt_part = jnp.dot(latent_low, dec_weight, preferred_element_type=jnp.float32)
-    rebuilt = lax.psum(rebuilt_part, ("latent", "row"))
+    rebuilt = lax.psum(lax.psum(rebuilt_part, "row"), "latent")
     grad_rows = 2.0 * (rebuilt + dec_bias - token_rows.astype(jnp.float32)) / total_rows
     grad_low = grad_rows.astype(jnp.bfloat16)
     dec_main = contract_rows(latent_low, grad_low)

time: 466 us -> 525 us (1.13)
  waiting for transfers between devices: 312 us -> 371 us
    psum x1 -> x2, waiting for transfers between devices: 63.5 us -> 122 us  [local(): rebuilt = lax.psum(lax.psum(rebuilt_part, 'row'), 'latent')]
  transfers between devices with their start and end apart: 7 -> 8, of which waited for: 6 -> 7; matrix products, arithmetic and copies ran while one was open for 14% -> 12% of each run, Pallas kernels for 0% -> 0%
where the time goes in v1:
time: 525 us; the launch traced here: 523 us
  waiting for transfers between devices  371 us (71%)
  matrix products  69.3 us (13%)
  local copies, waits for them, and re-layouts  54 us (10%)
  other arithmetic  14.3 us (3%)
  between operations  14.2 us (3%)
    psum x2, waiting for transfers between devices, local(): rebuilt = lax.psum(lax.psum(rebuilt_part, 'row'), 'latent')  122 us
    reduce_scatter x1, waiting for transfers between devices, local(): lax.psum_scatter(back_part, 'expert', scatter_dimension=0, tiled=True)  73.2 us
    reduce_scatter x1, waiting for transfers between devices, local(): lax.psum_scatter(preact_part, 'expert', scatter_dimension=0, tiled=True)  69.2 us
    unnamed x20, local copies, waits for them, and re-layouts  54 us
    dot_general x2, matrix products, contract_rows(): lax.dot_general(left, right, (((0,), (0,)), ((), ())), preferred_element_...  43.4 us
    psum x1, waiting for transfers between devices, local(): norm_sq = lax.psum(partial_sq[:, None] * column_pick[None, :], 'expert')  43.2 us
    all_gather x1, waiting for transfers between devices, local(): lax.all_gather(jnp.maximum(preact, 0.0).astype(jnp.bfloat16), 'expert', a...  36.9 us
    all_gather x1, waiting for transfers between devices, local(): token_rows = lax.all_gather(model_acts, 'row', axis=0, tiled=True)  25.6 us
  transfers between devices with their start and end apart: 8, of which 7 were waited for; matrix products, arithmetic and copies ran while one was open for 12% of the time, Pallas kernels for 0%

profile of v1, /device:TPU:0, one launch (start us, length us, event | category | flops | bytes accessed | tf_op | source)
XLA Modules:
  0.0 523.2 jit_solution(6685931923984663577)
XLA Ops:
  7.9 25.6 %all-gather.4.cloned.1.call-done = bf16[512,1024]{1,0:T(8,128)(2,1)} async-done(((bf16[256,1024]{1,0:T(8,128)(2,1)}), bf16[512,1024]{1,0:T(8,128)(2,1)}) %all-gather.4.cloned.1.call-update) | async-done | bytes 1048592 | tf_op jit(solution)/shard_map/all_gather | solution.py:52
  33.6 9.2 %fusion.14 = f32[512,3072]{1,0:T(8,128)} fusion(bf16[512,1024]{1,0:T(8,128)(2,1)} %all-gather.4.cloned.1.call-done, bf16[1024,3072]{1,0:T(8,128)(2,1)} %param.10), kind=kOutput, calls=%fused_computation.33 | convolution fusion | flops 3221225472 | bytes 13631488 | tf_op jit(solution)/shard_map/dot_general | solution.py:63
  43.5 69.2 %reduce-scatter.3.cloned.1.call-done = f32[64,3072]{1,0:T(8,128)} async-done(((f32[512,3072]{1,0:T(8,128)}), f32[64,3072]{1,0:T(8,128)}) %reduce-scatter.3.cloned.1.call-update) | async-done | bytes 786448 | tf_op jit(solution)/shard_map/reduce_scatter | solution.py:64
  112.7 1.9 maximum_convert_fusion
  114.7 36.9 %all-gather.6.cloned.1.call-done = bf16[512,3072]{1,0:T(8,128)(2,1)} async-done(((bf16[64,3072]{1,0:T(8,128)(2,1)}), bf16[512,3072]{1,0:T(8,128)(2,1)}) %all-gather.6.cloned.1.call-update) | async-done | bytes 3145744 | tf_op jit(solution)/shard_map/all_gather | solution.py:66
  151.7 8.5 %fusion.15 = f32[512,1024]{1,0:T(8,128)} fusion(bf16[512,3072]{1,0:T(8,128)(2,1)} %all-gather.6.cloned.1.call-done, bf16[3072,1024]{1,0:T(8,128)(2,1)} %param.11), kind=kOutput, calls=%fused_computation.34 | convolution fusion | flops 3221225472 | bytes 11534336 | tf_op jit(solution)/shard_map/dot_general | solution.py:69
  160.2 62.0 %all-reduce.4.cloned.1.call-done = f32[512,1024]{1,0:T(8,128)} async-done(((f32[512,1024]{1,0:T(8,128)}), f32[512,1024]{1,0:T(8,128)}) %all-reduce.4.cloned.1.call-update) | async-done | bytes 2097168 | tf_op jit(solution)/shard_map/psum | solution.py:70
  222.3 4.1 fusion
  227.2 60.2 %all-reduce.6.cloned.1.call-done = f32[512,1024]{1,0:T(8,128)} async-done(((f32[512,1024]{1,0:T(8,128)}), f32[512,1024]{1,0:T(8,128)}) %all-reduce.6.cloned.1.call-update) | async-done | bytes 2097168 | tf_op jit(solution)/shard_map/psum | solution.py:70
  287.3 2.6 fusion.11
  290.9 8.2 %fusion.16 = f32[512,3072]{1,0:T(8,128)} fusion(bf16[512,1024]{1,0:T(8,128)(2,1)S(1)} %get-tuple-element.33, bf16[3072,1024]{1,0:T(8,128)(2,1)} %param.11), kind=kOutput, calls=%fused_computation.35 | convolution fusion | flops 3221225472 | bytes 13631488 | tf_op jit(solution)/shard_map/dot_general | solution.py:76
  299.2 43.2 %all-reduce.8.cloned.1.call-done = f32[3072,8]{0,1:T(8,128)} async-done(((f32[3072,8]{0,1:T(8,128)}), f32[3072,8]{0,1:T(8,128)}) %all-reduce.8.cloned.1.call-update) | async-done | bytes 98320 | tf_op jit(solution)/shard_map/psum | solution.py:59
  342.5 1.0 multiply_reduce_fusion
  343.5 73.2 %reduce-scatter.5.cloned.1.call-done = f32[64,3072]{1,0:T(8,128)} async-done(((f32[512,3072]{1,0:T(8,128)}), f32[64,3072]{1,0:T(8,128)}) %reduce-scatter.5.cloned.1.call-update) | async-done | bytes 786448 | tf_op jit(solution)/shard_map/reduce_scatter | solution.py:80
  416.7 2.0 select_convert_fusion
  418.7 8.9 %copy.23 = bf16[1024,3072]{0,1:T(8,128)(2,1)} copy(bf16[1024,3072]{1,0:T(8,128)(2,1)} %param.10) | data formatting | bytes 12582912 | tf_op args[1]
  427.6 8.6 %copy.24 = bf16[1024,3072]{0,1:T(8,128)(2,1)} copy(bf16[1024,3072]{1,0:T(8,128)(2,1)} %param.14) | data formatting | bytes 12582912 | tf_op args[5]
  436.3 8.8 %copy.25 = bf16[1024,3072]{0,1:T(8,128)(2,1)} copy(bf16[1024,3072]{1,0:T(8,128)(2,1)} %param.15) | data formatting | bytes 12582912 | tf_op args[6]
  445.7 21.2 %fusion.9 = (bf16[3072,1024]{1,0:T(8,128)(2,1)}, bf16[3072,1024]{1,0:T(8,128)(2,1)}, bf16[3072,1024]{1,0:T(8,128)(2,1)}) fusion(bf16[3072,1024]{1,0:T(8,128)(2,1)} %param.17, bf16[3072,1024]{1,0:T(8,128)(2,1)} %param.16, bf16[3072,1024]{1,0:T(8,128)(2,1)} %param.11, f32[3072]{0:T(1024)S(1)} %get-tuple-element.24, f32[3072]{0:T(1024)S(1)} %broadcast_multiply_fusion.1, ...), kind=kOutput, calls=%fused_computation.17 | convolution fusion | flops 3287285760 | bytes 41967616 | tf_op jit(solution)/shard_map/dot_general | solution.py:32
  467.0 22.1 %fusion.10 = (bf16[1024,3072]{0,1:T(8,128)(2,1)}, bf16[1024,3072]{0,1:T(8,128)(2,1)}, bf16[1024,3072]{0,1:T(8,128)(2,1)}) fusion(bf16[1024,3072]{0,1:T(8,128)(2,1)} %copy.25, bf16[1024,3072]{0,1:T(8,128)(2,1)} %copy.24, bf16[1024,3072]{0,1:T(8,128)(2,1)} %copy.23, bf16[512,3072]{1,0:T(8,128)(2,1)} %all-gather.8.cloned.1.call-done, ...), kind=kOutput, calls=%fused_computation.18 | convolution fusion | flops 3277848576 | bytes 41943040 | tf_op jit(solution)/shard_map/dot_general | solution.py:32
  489.1 8.6 %copy.28 = bf16[1024,3072]{1,0:T(8,128)(2,1)} copy(bf16[1024,3072]{0,1:T(8,128)(2,1)} %get-tuple-element.29) | data formatting | bytes 12582912
  497.7 8.6 %copy.26 = bf16[1024,3072]{1,0:T(8,128)(2,1)} copy(bf16[1024,3072]{0,1:T(8,128)(2,1)} %get-tuple-element.30) | data formatting | bytes 12582912
  506.3 8.8 %copy.27 = bf16[1024,3072]{1,0:T(8,128)(2,1)} copy(bf16[1024,3072]{0,1:T(8,128)(2,1)} %get-tuple-element.31) | data formatting | bytes 12582912
  515.1 1.2 convert_reduce_fusion
  (37 shorter events, 4.1 us)
Async XLA Ops:
  7.2 26.4 %all-gather.4.cloned.1.call-start = ((), (), s32[]{:S(2)}) async-start(), calls=%async_computation.2 | async-start | bytes 1572864 | tf_op jit(solution)/shard_map/all_gather | solution.py:52
  7.9 104.8 %reduce-scatter.3.cloned.1.call-start = ((), (), s32[]{:S(2)}) async-start(), calls=%async_computation.3 | async-start | bytes 7077888 | tf_op jit(solution)/shard_map/reduce_scatter | solution.py:64
  42.8 0.7 copy-start.5
  42.8 108.8 %all-gather.6.cloned.1.call-start = ((), (), s32[]{:S(2)}) async-start(), calls=%async_computation.4 | async-start | bytes 3538944 | tf_op jit(solution)/shard_map/all_gather | solution.py:66
  114.7 107.5 %all-reduce.4.cloned.1.call-start = ((), (), s32[]{:S(2)}) async-start(), calls=%async_computation.5 | async-start | bytes 4194304 | tf_op jit(solution)/shard_map/psum | solution.py:70
  160.1 127.2 %copy-start.3 = (bf16[512,1024]{1,0:T(8,128)(2,1)S(1)}, bf16[512,1024]{1,0:T(8,128)(2,1)}, u32[]{:S(2)}) copy-start(bf16[512,1024]{1,0:T(8,128)(2,1)} %all-gather.4.cloned.1.call-done) | copy-start | bytes 3145732
  160.1 127.2 %copy-start.6 = (f32[1024]{0:T(1024)S(1)}, f32[1024]{0:T(1024)}, u32[]{:S(2)}) copy-start(f32[1024]{0:T(1024)} %param.13) | copy-start | bytes 12292
  160.2 127.2 %all-reduce.6.cloned.1.call-start = ((), (), s32[]{:S(2)}) async-start(), calls=%async_computation.6 | async-start | bytes 4194304 | tf_op jit(solution)/shard_map/psum | solution.py:70
  222.2 120.3 %all-reduce.8.cloned.1.call-start = ((), (), s32[]{:S(2)}) async-start(), calls=%async_computation.8 | async-start | bytes 196608 | tf_op jit(solution)/shard_map/psum | solution.py:59
  227.1 189.6 %reduce-scatter.5.cloned.1.call-start = ((), (), s32[]{:S(2)}) async-start(), calls=%async_computation.7 | async-start | bytes 7077888 | tf_op jit(solution)/shard_map/reduce_scatter | solution.py:80
  290.0 1.0 copy-start.4
  299.2 117.5 %copy-start.2 = (f32[64,3072]{1,0:T(8,128)S(1)}, f32[64,3072]{1,0:T(8,128)}, u32[]{:S(2)}) copy-start(f32[64,3072]{1,0:T(8,128)} %reduce-scatter.3.cloned.1.call-done) | copy-start | bytes 2359300
  299.2 167.8 %all-gather.8.cloned.1.call-start = ((), (), s32[]{:S(2)}) async-start(), calls=%async_computation.9 | async-start | bytes 3538944 | tf_op jit(solution)/shard_map/all_gather | solution.py:81
  436.3 8.8 %copy-start = (bf16[512,3072]{1,0:T(8,128)(2,1)S(1)}, bf16[512,3072]{1,0:T(8,128)(2,1)}, u32[]{:S(2)}) copy-start(bf16[512,3072]{1,0:T(8,128)(2,1)} %all-gather.6.cloned.1.call-done) | copy-start | bytes 9437188
  506.3 8.8 %copy-start.1 = (bf16[512,3072]{1,0:T(8,128)(2,1)S(1)}, bf16[512,3072]{1,0:T(8,128)(2,1)}, u32[]{:S(2)}) copy-start(bf16[512,3072]{1,0:T(8,128)(2,1)} %all-gather.8.cloned.1.call-done) | copy-start | bytes 9437188
Sparse Core Ops, SparseCore 0:
  9.5 23.9 all-gather.3
  42.9 69.7 reduce-scatter.2
  114.9 36.6 all-gather.5
  160.3 61.8 all-reduce.3
  224.3 62.9 all-reduce.5
  290.1 52.3 all-reduce.7
  345.3 71.3 reduce-scatter.4
  418.8 36.6 all-gather.7
